TPU v7x, 32 devices: a whole 2x2x4 slice. The times are simulated.
32 devices in a mesh: grp: 4 (over y, x), own: 8 (over z, core).
Axes of the slice: x: 2, y: 2, z: 4, core: 2. Of those that a mesh axis runs over, the one named last changes fastest.
Arguments:
- tile_row: int32 [4, 8, 1536], P('grp', 'own'), may hold values from 0 to 7
- pixel_col: int32 [4, 8, 1536], P('grp', 'own'), may hold values from 0 to 16383
- weight: bfloat16 [4, 8, 1536], P('grp', 'own'), may hold values from 0.25 to 4
- counts: int32 [4, 8, 8], P('grp', 'own'), may hold values from 1 to 192
- kernel: float32 [9, 9], replicated, may hold values from 0.01 to 0.05
Outputs:
- smoothed: float32 [64, 16384], P('own', 'grp')
Inputs may be any that keep to these rules, and one draw needn't show every extreme that they name: `counts`: slots past a block's count hold unused values.
All inputs are finite; a program needn't handle non-finite values.
Results may differ from a plain program's by a relative error of at most 0.0012.
Values may be sent and summed in bfloat16 or wider, within the bound.
A program may use at most 64 MiB of HBM per device.

v0:
```python
import jax
import jax.numpy as jnp
from jax import lax
from jax.sharding import PartitionSpec as P

W = 16384
STRIP = 8


def extended(cells, sides, width):
    for axis, dim in sides:
        count = lax.axis_size(axis)
        ends = count - 1
        head = lax.slice_in_dim(cells, 0, width, axis=dim)
        tail = lax.slice_in_dim(cells, cells.shape[dim] - width, cells.shape[dim], axis=dim)
        cells = jnp.concatenate(
            [
                lax.ppermute(tail, axis, [(i, (i + 1) % count) for i in range(ends)]),
                cells,
                lax.ppermute(head, axis, [((i + 1) % count, i) for i in range(ends)]),
            ],
            axis=dim,
        )
    return cells


def bin_points(packed, masses, col_span):
    row_ids = packed // col_span
    col_ids = packed % col_span
    groups = col_span // 128
    cell_count = STRIP * groups
    cell_index = row_ids * groups + col_ids // 128
    lane_index = col_ids % 128
    slot_count = cell_index.shape[0]
    block_len = max(1, min(slot_count, 2**21 // cell_count))
    block_count = -(-slot_count // block_len)
    cell_iota = lax.broadcasted_iota(jnp.int32, (cell_count, 1), 0)
    lane_iota = lax.broadcasted_iota(jnp.int32, (1, 128), 1)

    def add_block(i, running):
        cells_here = lax.dynamic_slice_in_dim(cell_index, i * block_len, block_len)
        lanes_here = lax.dynamic_slice_in_dim(lane_index, i * block_len, block_len)
        masses_here = lax.dynamic_slice_in_dim(masses, i * block_len, block_len)
        onehot_cells = (cell_iota == cells_here[None, :]).astype(jnp.bfloat16)
        onehot_lanes = jnp.where(
            lane_iota == lanes_here[:, None], masses_here[:, None], jnp.zeros((), jnp.bfloat16)
        )
        return running + jnp.dot(onehot_cells, onehot_lanes, preferred_element_type=jnp.float32)

    running = lax.fori_loop(0, block_count, add_block, jnp.zeros((cell_count, 128), jnp.float32))
    return running.reshape(STRIP, col_span)


def per_device(tile_row, pixel_col, weight, counts, kernel):
    owners = lax.axis_size("own")
    group_count = lax.axis_size("grp")
    cap_len = tile_row.shape[2] // owners
    tile_rows = tile_row.reshape(owners, cap_len)
    columns = pixel_col.reshape(owners, cap_len)
    masses = weight.reshape(owners, cap_len)
    live = lax.broadcasted_iota(jnp.int32, (owners, cap_len), 1) < counts.reshape(owners, 1)
    masses = jnp.where(live, masses, jnp.zeros((), jnp.bfloat16))
    quarter_cols = W // group_count
    bands = lax.broadcasted_iota(jnp.int32, (group_count, 1, 1), 0)
    in_band = columns[None] // quarter_cols == bands
    sent_masses = jnp.where(in_band, masses[None], jnp.zeros((), jnp.bfloat16))
    band_cols = jnp.clip(columns[None] - bands * quarter_cols, 0, quarter_cols - 1)
    sent_index = tile_rows[None] * quarter_cols + band_cols
    got_index, got_masses = (
        lax.all_to_all(
            lax.all_to_all(sent_index, "grp", split_axis=0, concat_axis=0, tiled=True),
            "own",
            split_axis=1,
            concat_axis=1,
            tiled=True,
        ),
        lax.all_to_all(
            lax.all_to_all(sent_masses, "grp", split_axis=0, concat_axis=0, tiled=True),
            "own",
            split_axis=1,
            concat_axis=1,
            tiled=True,
        ),
    )
    quarter = bin_points(got_index.reshape(-1), got_masses.reshape(-1), quarter_cols)
    framed = extended(quarter.astype(jnp.bfloat16), (("own", 0), ("grp", 1)), 4).astype(
        quarter.dtype
    )
    smoothed = jnp.zeros((STRIP, quarter_cols), jnp.float32)
    for a in range(9):
        for b in range(9):
            smoothed = smoothed + kernel[a, b] * framed[a : a + STRIP, b : b + quarter_cols]
    return smoothed


def solution(mesh):
    placed = (
        P("grp", "own", None),
        P("grp", "own", None),
        P("grp", "own", None),
        P("grp", "own", None),
        P(),
    )
    return jax.shard_map(
        per_device, mesh=mesh, in_specs=placed, out_specs=P("own", "grp"), check_vma=False
    )
```

profile of v0, /device:TPU:1, one launch (start us, length us, event | category | flops | bytes accessed | tf_op | source)
XLA Modules:
  0.0 110.8 jit_solution(12894617945058274313)
XLA Ops:
  0.0 0.7 reduce.1
  0.8 0.7 reduce.2
  1.5 0.1 reshape.209
  1.6 0.7 fusion.97
  2.4 0.6 fusion.90
  3.0 4.3 %all-to-all-start.2 = ((bf16[4,8,192]{2,1,0:T(8,128)(2,1)}), bf16[4,8,192]{2,1,0:T(8,128)(2,1)S(1)}, u32[]{:S(2)}, u32[]{:S(2)}) async-start(bf16[4,8,192]{2,1,0:T(8,128)(2,1)} %fusion.90), calls=%async_computation.2 | async-start | bytes 32768 | tf_op jit(solution)/shard_map/all_to_all | solution.py:78
  7.2 0.7 multiply_reduce_fusion
  8.0 0.7 clamp_add_fusion
  8.7 2.1 %all-to-all-done.2 = bf16[4,8,192]{2,1,0:T(8,128)(2,1)S(1)} async-done(((bf16[4,8,192]{2,1,0:T(8,128)(2,1)}), bf16[4,8,192]{2,1,0:T(8,128)(2,1)S(1)}, u32[]{:S(2)}, u32[]{:S(2)}) %all-to-all-start.2) | async-done | bytes 12320 | tf_op jit(solution)/shard_map/all_to_all | solution.py:78
  10.8 3.3 %all-to-all-start = ((s32[4,8,192]{2,1,0:T(8,128)}), s32[4,8,192]{2,1,0:T(8,128)S(1)}, u32[]{:S(2)}, u32[]{:S(2)}) async-start(s32[4,8,192]{2,1,0:T(8,128)} %clamp_add_fusion), calls=%async_computation | async-start | bytes 65536 | tf_op jit(solution)/shard_map/all_to_all | solution.py:71
  14.1 0.7 fusion.102
  14.8 0.6 copy.10
  15.4 2.2 %all-to-all-done = s32[4,8,192]{2,1,0:T(8,128)S(1)} async-done(((s32[4,8,192]{2,1,0:T(8,128)}), s32[4,8,192]{2,1,0:T(8,128)S(1)}, u32[]{:S(2)}, u32[]{:S(2)}) %all-to-all-start) | async-done | bytes 24608 | tf_op jit(solution)/shard_map/all_to_all | solution.py:71
  17.6 8.1 %all-to-all-start.3 = ((bf16[4,8,192]{2,0,1:T(4,128)(2,1)}), bf16[4,8,192]{2,0,1:T(4,128)(2,1)S(1)}, u32[]{:S(2)}, u32[]{:S(2)}) async-start(bf16[4,8,192]{2,0,1:T(4,128)(2,1)} %copy.10), calls=%async_computation.3 | async-start | bytes 32768 | tf_op jit(solution)/shard_map/all_to_all | solution.py:77
  25.7 0.7 fusion.101
  26.5 0.6 copy.8
  27.1 3.6 %all-to-all-done.3 = bf16[4,8,192]{2,0,1:T(4,128)(2,1)S(1)} async-done(((bf16[4,8,192]{2,0,1:T(4,128)(2,1)}), bf16[4,8,192]{2,0,1:T(4,128)(2,1)S(1)}, u32[]{:S(2)}, u32[]{:S(2)}) %all-to-all-start.3) | async-done | bytes 12320 | tf_op jit(solution)/shard_map/all_to_all | solution.py:77
  30.7 4.0 %all-to-all-start.1 = ((s32[4,8,192]{2,0,1:T(4,128)}), s32[4,8,192]{2,0,1:T(4,128)S(1)}, u32[]{:S(2)}, u32[]{:S(2)}) async-start(s32[4,8,192]{2,0,1:T(4,128)} %copy.8), calls=%async_computation.1 | async-start | bytes 65536 | tf_op jit(solution)/shard_map/all_to_all | solution.py:70
  34.7 0.7 fusion.103
  35.4 0.1 broadcast_in_dim.45
  35.5 4.2 %all-to-all-done.1 = s32[4,8,192]{2,0,1:T(4,128)S(1)} async-done(((s32[4,8,192]{2,0,1:T(4,128)}), s32[4,8,192]{2,0,1:T(4,128)S(1)}, u32[]{:S(2)}, u32[]{:S(2)}) %all-to-all-start.1) | async-done | bytes 24608 | tf_op jit(solution)/shard_map/all_to_all | solution.py:70
  39.8 1.9 %fusion.5 = bf16[256,128]{1,0:T(8,128)(2,1)S(1)} fusion(s32[6144]{0:T(1024)S(1)} %get-tuple-element.32, s32[6144]{0:T(1024)S(1)} %get-tuple-element.23, bf16[6144]{0:T(1024)(128)(2,1)S(1)} %broadcast_in_dim.45), kind=kOutput, calls=%fused_computation.6 | convolution fusion | flops 405831680 | bytes 126976 | tf_op jit(solution)/shard_map/while/body/eval_jaxpr/dot_general | solution.py:48
  41.8 2.9 %collective-permute-start = (bf16[4,4096]{1,0:T(4,128)(2,1)S(1)}, bf16[4,4096]{1,0:T(4,128)(2,1)S(1)}, u32[]{:S(2)}, u32[]{:S(2)}) collective-permute-start(bf16[4,4096]{1,0:T(4,128)(2,1)S(1)} %slice.506), channel_id=1, source_target_pairs={{0,1},{1,2},{2,3},{3,4},{4,5},{5,6},{6,7},{8,9},{9,10},{10,11},{11... | collective-permute-start | bytes 98312 | tf_op jit(solution)/shard_map/ppermute | solution.py:18
  44.7 1.9 %collective-permute-start.1 = (bf16[4,4096]{1,0:T(4,128)(2,1)S(1)}, bf16[4,4096]{1,0:T(4,128)(2,1)S(1)}, u32[]{:S(2)}, u32[]{:S(2)}) collective-permute-start(bf16[4,4096]{1,0:T(4,128)(2,1)S(1)} %slice.508), channel_id=1, source_target_pairs={{1,0},{2,1},{3,2},{4,3},{5,4},{6,5},{7,6},{9,8},{10,9},{11,10},{12... | collective-permute-start | bytes 98312 | tf_op jit(solution)/shard_map/ppermute | solution.py:20
  46.7 0.7 fusion.104
  47.4 2.5 %collective-permute-done.1 = bf16[4,4096]{1,0:T(4,128)(2,1)S(1)} collective-permute-done((bf16[4,4096]{1,0:T(4,128)(2,1)S(1)}, bf16[4,4096]{1,0:T(4,128)(2,1)S(1)}, u32[]{:S(2)}, u32[]{:S(2)}) %collective-permute-start.1) | collective-permute-done | bytes 32800 | tf_op jit(solution)/shard_map/ppermute | solution.py:20
  50.1 2.3 %collective-permute-start.2 = (bf16[16,4]{1,0:T(8,128)(2,1)S(1)}, bf16[16,4]{1,0:T(8,128)(2,1)S(1)}, u32[]{:S(2)}, u32[]{:S(2)}) collective-permute-start(bf16[16,4]{1,0:T(8,128)(2,1)S(1)} %get-tuple-element.20), channel_id=1, source_target_pairs={{0,8},{8,16},{16,24},{1,9},{9,17},{17,25},{2,10},{10,18},{18,26},{... | collective-permute-start | bytes 392 | tf_op jit(solution)/shard_map/ppermute | solution.py:18
  52.4 1.3 %collective-permute-start.3 = (bf16[16,4]{1,0:T(8,128)(2,1)S(1)}, bf16[16,4]{1,0:T(8,128)(2,1)S(1)}, u32[]{:S(2)}, u32[]{:S(2)}) collective-permute-start(bf16[16,4]{1,0:T(8,128)(2,1)S(1)} %get-tuple-element.19), channel_id=1, source_target_pairs={{8,0},{16,8},{24,16},{9,1},{17,9},{25,17},{10,2},{18,10},{26,18},{... | collective-permute-start | bytes 392 | tf_op jit(solution)/shard_map/ppermute | solution.py:20
  53.7 0.7 fusion.105
  54.3 2.4 %collective-permute-done.3 = bf16[16,4]{1,0:T(8,128)(2,1)S(1)} collective-permute-done((bf16[16,4]{1,0:T(8,128)(2,1)S(1)}, bf16[16,4]{1,0:T(8,128)(2,1)S(1)}, u32[]{:S(2)}, u32[]{:S(2)}) %collective-permute-start.3) | collective-permute-done | bytes 160 | tf_op jit(solution)/shard_map/ppermute | solution.py:20
  56.7 0.2 concatenate.7
  56.9 53.9 %fusion.10 = f32[8,4096]{1,0:T(8,128)} fusion(f32[16,4104]{1,0:T(8,128)S(1)} %convert_element_type.13, f32[]{:T(128)} %bitcast.81, f32[]{:T(128)} %bitcast.80, f32[]{:T(128)} %bitcast.79, f32[]{:T(128)} %bitcast.78, f32[]{:T(128)} %bitcast.77, f32[]{:T(128)} %bitcast.76, f32[]{:T(128)} %bitcast.75, f32[]{:T(128)} %bitcast.74, f32[]{:T(128)} %bitcast.73, ...), kind=kLoop, calls=%fused_computation.10 | loop fusion | flops 5275648 | bytes 10748228 | tf_op jit(solution)/shard_map/add | solution.py:92
  (19 shorter events, 0.5 us)
Async XLA Ops:
  0.0 14.0 %copy-start = (f32[9,9]{1,0:T(8,128)S(1)}, f32[9,9]{1,0:T(8,128)}, u32[]{:S(2)}) copy-start(f32[9,9]{1,0:T(8,128)} %param.9) | copy-start | bytes 976
  3.0 7.8 %all-to-all-start.2 = ((bf16[4,8,192]{2,1,0:T(8,128)(2,1)}), bf16[4,8,192]{2,1,0:T(8,128)(2,1)S(1)}, u32[]{:S(2)}, u32[]{:S(2)}) async-start(bf16[4,8,192]{2,1,0:T(8,128)(2,1)} %fusion.90), calls=%async_computation.2 | async-start | bytes 32768 | tf_op jit(solution)/shard_map/all_to_all | solution.py:78
  10.8 6.8 %all-to-all-start = ((s32[4,8,192]{2,1,0:T(8,128)}), s32[4,8,192]{2,1,0:T(8,128)S(1)}, u32[]{:S(2)}, u32[]{:S(2)}) async-start(s32[4,8,192]{2,1,0:T(8,128)} %clamp_add_fusion), calls=%async_computation | async-start | bytes 65536 | tf_op jit(solution)/shard_map/all_to_all | solution.py:71
  17.6 13.1 %all-to-all-start.3 = ((bf16[4,8,192]{2,0,1:T(4,128)(2,1)}), bf16[4,8,192]{2,0,1:T(4,128)(2,1)S(1)}, u32[]{:S(2)}, u32[]{:S(2)}) async-start(bf16[4,8,192]{2,0,1:T(4,128)(2,1)} %copy.10), calls=%async_computation.3 | async-start | bytes 32768 | tf_op jit(solution)/shard_map/all_to_all | solution.py:77
  30.7 9.0 %all-to-all-start.1 = ((s32[4,8,192]{2,0,1:T(4,128)}), s32[4,8,192]{2,0,1:T(4,128)S(1)}, u32[]{:S(2)}, u32[]{:S(2)}) async-start(s32[4,8,192]{2,0,1:T(4,128)} %copy.8), calls=%async_computation.1 | async-start | bytes 65536 | tf_op jit(solution)/shard_map/all_to_all | solution.py:70
  41.8 5.7 %collective-permute-start = (bf16[4,4096]{1,0:T(4,128)(2,1)S(1)}, bf16[4,4096]{1,0:T(4,128)(2,1)S(1)}, u32[]{:S(2)}, u32[]{:S(2)}) collective-permute-start(bf16[4,4096]{1,0:T(4,128)(2,1)S(1)} %slice.506), channel_id=1, source_target_pairs={{0,1},{1,2},{2,3},{3,4},{4,5},{5,6},{6,7},{8,9},{9,10},{10,11},{11... | collective-permute-start | bytes 98312 | tf_op jit(solution)/shard_map/ppermute | solution.py:18
  44.7 5.2 %collective-permute-start.1 = (bf16[4,4096]{1,0:T(4,128)(2,1)S(1)}, bf16[4,4096]{1,0:T(4,128)(2,1)S(1)}, u32[]{:S(2)}, u32[]{:S(2)}) collective-permute-start(bf16[4,4096]{1,0:T(4,128)(2,1)S(1)} %slice.508), channel_id=1, source_target_pairs={{1,0},{2,1},{3,2},{4,3},{5,4},{6,5},{7,6},{9,8},{10,9},{11,10},{12... | collective-permute-start | bytes 98312 | tf_op jit(solution)/shard_map/ppermute | solution.py:20
  50.1 4.2 %collective-permute-start.2 = (bf16[16,4]{1,0:T(8,128)(2,1)S(1)}, bf16[16,4]{1,0:T(8,128)(2,1)S(1)}, u32[]{:S(2)}, u32[]{:S(2)}) collective-permute-start(bf16[16,4]{1,0:T(8,128)(2,1)S(1)} %get-tuple-element.20), channel_id=1, source_target_pairs={{0,8},{8,16},{16,24},{1,9},{9,17},{17,25},{2,10},{10,18},{18,26},{... | collective-permute-start | bytes 392 | tf_op jit(solution)/shard_map/ppermute | solution.py:18
  52.4 4.4 %collective-permute-start.3 = (bf16[16,4]{1,0:T(8,128)(2,1)S(1)}, bf16[16,4]{1,0:T(8,128)(2,1)S(1)}, u32[]{:S(2)}, u32[]{:S(2)}) collective-permute-start(bf16[16,4]{1,0:T(8,128)(2,1)S(1)} %get-tuple-element.19), channel_id=1, source_target_pairs={{8,0},{16,8},{24,16},{9,1},{17,9},{25,17},{10,2},{18,10},{26,18},{... | collective-permute-start | bytes 392 | tf_op jit(solution)/shard_map/ppermute | solution.py:20
where the time goes:
time: 112 us; the launch traced here: 111 us
  other arithmetic  58.2 us (52%)
  starting transfers between devices  28 us (25%)
  waiting for transfers between devices  17 us (15%)
  local copies, waits for them, and re-layouts  5.53 us (5%)
  matrix products  1.92 us (2%)
    add x1, other arithmetic, per_device(): smoothed = smoothed + kernel[a, b] * framed[a:a + STRIP, b:b + quarter_cols]  53.9 us
    all_to_all x1, starting transfers between devices, per_device(): lax.all_to_all(lax.all_to_all(sent_masses, 'grp', split_axis=0, concat_ax...  8.13 us
    ppermute x2, starting transfers between devices, extended(): lax.ppermute(tail, axis, [(i, (i + 1) % count) for i in range(ends)])  5.21 us
    ppermute x2, waiting for transfers between devices, extended(): lax.ppermute(head, axis, [((i + 1) % count, i) for i in range(ends)])  4.91 us
    all_to_all x1, starting transfers between devices, per_device(): lax.all_to_all(sent_masses, 'grp', split_axis=0, concat_axis=0, tiled=True)  4.25 us
    all_to_all x1, waiting for transfers between devices, per_device(): lax.all_to_all(lax.all_to_all(sent_index, 'grp', split_axis=0, concat_axi...  4.17 us
    all_to_all x1, starting transfers between devices, per_device(): lax.all_to_all(lax.all_to_all(sent_index, 'grp', split_axis=0, concat_axi...  3.98 us
    all_to_all x1, waiting for transfers between devices, per_device(): lax.all_to_all(lax.all_to_all(sent_masses, 'grp', split_axis=0, concat_ax...  3.58 us
  transfers between devices with their start and end apart: 8, of which 6 were waited for; matrix products, arithmetic and copies ran while one was open for 6% of the time, Pallas kernels for 0%

commit v1 on v0

v1 whole, which is shorter than its diff:
```python
import functools
import math

import jax
import jax.numpy as jnp
from jax import lax
from jax.experimental import pallas as pl
from jax.experimental.pallas import tpu as pltpu
from jax.sharding import PartitionSpec as P

W = 16384
STRIP = 8
REACH = 4
TAPS = 9
LANES = 256
CHUNK = 512
BATCH = 4
MESH = pl.DeviceIdType.MESH


def heat_kernel(
    n_g, n_o, cap, span, row_ref, col_ref, weight_ref, counts_ref, kern_ref, out_ref,
    stage, recv, acc, halo_out, halo_in, ext,
    send_sem, recv_sem, halo_send_sem, halo_recv_sem,
):
    n = n_g * n_o
    me_g, me_o = lax.axis_index("grp"), lax.axis_index("own")
    me = me_g * n_o + me_o
    quarter = out_ref.shape[1]
    slots = row_ref.shape[2]
    tiles = acc.shape[0] // STRIP

    barrier = pltpu.get_barrier_semaphore()

    def greet(k, carry):
        peer = lax.rem(me + k, n)
        pl.semaphore_signal(
            barrier, inc=1, device_id=(lax.div(peer, n_o), lax.rem(peer, n_o)), device_id_type=MESH
        )
        return carry

    lax.fori_loop(1, n, greet, 0)

    period = math.lcm(cap, 128)
    per = period // cap

    def prepare(k, carry):
        at = pl.ds(pl.multiple_of(k * period, 128), period)
        lane = lax.broadcasted_iota(jnp.int32, (1, period), 1)
        limit = jnp.full((1, period), counts_ref[0, 0, k * per], jnp.int32)
        for j in range(1, per):
            limit = jnp.where(lane >= j * cap, counts_ref[0, 0, k * per + j] + j * cap, limit)
        index = row_ref[0, :, at] * W + col_ref[0, :, at]
        stage[0:1, at] = index.astype(jnp.float32)
        stage[1:2, at] = jnp.where(lane < limit, weight_ref[0, :, at].astype(jnp.float32), 0.0)
        return carry

    lax.fori_loop(0, slots // period, prepare, 0)
    for k in range(halo_in.shape[0]):
        halo_in_zero = jnp.zeros(halo_in.shape[1:], halo_in.dtype)

        @pl.when(me_o == (0 if k == 0 else n_o - 1))
        def _():
            halo_in[k] = halo_in_zero

    acc[...] = jnp.zeros_like(acc)

    def window(owner):
        return pl.ds(pl.multiple_of(lax.div(owner * cap, 128) * 128, 128), span)

    def copy_to(k):
        peer = lax.rem(me + k, n)
        peer_g, peer_o = lax.div(peer, n_o), lax.rem(peer, n_o)
        return pltpu.make_async_remote_copy(
            src_ref=stage.at[:, window(peer_o)],
            dst_ref=recv.at[me],
            send_sem=send_sem.at[k],
            recv_sem=recv_sem.at[me],
            device_id=(peer_g, peer_o),
            device_id_type=MESH,
        )

    def copy_from(k):
        src = lax.rem(me + k, n)
        return pltpu.make_async_remote_copy(
            src_ref=stage.at[:, window(me_o)],
            dst_ref=recv.at[src],
            send_sem=send_sem.at[k],
            recv_sem=recv_sem.at[src],
            device_id=(lax.div(src, n_o), lax.rem(src, n_o)),
            device_id_type=MESH,
        )

    pl.semaphore_wait(barrier, n - 1)

    def send(k, carry):
        copy_to(k).start()
        return carry

    lax.fori_loop(1, n, send, 0)
    recv[me] = stage[:, window(me_o)]

    offset = lax.rem(me_o * cap, 128)
    first_col = me_g * quarter - REACH

    def onehots(points):
        index = points[0:1].astype(jnp.int32)
        place = lax.broadcasted_iota(jnp.int32, (1, span), 1) - offset
        reach = (index & (W - 1)) - first_col
        used = (place >= 0) & (place < cap) & (reach >= 0) & (reach < quarter + 2 * REACH)
        mass = jnp.where(used, points[1:2], 0.0)
        cell = (reach // LANES) * STRIP + index // W
        lane = reach & (LANES - 1)
        cell_iota = lax.broadcasted_iota(jnp.int32, (acc.shape[0], span), 0)
        lane_iota = lax.broadcasted_iota(jnp.int32, (LANES, span), 0)
        cells = jnp.where(cell_iota == cell, 1.0, 0.0).astype(jnp.bfloat16)
        lanes = jnp.where(lane_iota == lane, mass, 0.0).astype(jnp.bfloat16)
        return cells, lanes

    def bin_batch(t, carry):
        cells, lanes = [], []
        for u in range(BATCH):
            k = t * BATCH + u

            @pl.when(k > 0)
            def _():
                copy_from(k).wait_recv()

        for u in range(BATCH):
            a, b = onehots(recv[lax.rem(me + t * BATCH + u, n)])
            cells.append(a)
            lanes.append(b)
        acc[...] += lax.dot_general(
            jnp.concatenate(cells, axis=1),
            jnp.concatenate(lanes, axis=1),
            (((1,), (1,)), ((), ())),
            preferred_element_type=jnp.float32,
        )
        return carry

    lax.fori_loop(0, n // BATCH, bin_batch, 0)

    for t in range(tiles):
        at = pl.ds(t * LANES, LANES)
        heat = acc[t * STRIP : (t + 1) * STRIP, :]
        halo_out[0, :, at] = heat[STRIP - REACH :].astype(jnp.bfloat16)
        halo_out[1, :, at] = heat[:REACH].astype(jnp.bfloat16)
        ext[REACH : REACH + STRIP, at] = heat

    def halo_copy(side, owner):
        return pltpu.make_async_remote_copy(
            src_ref=halo_out.at[side],
            dst_ref=halo_in.at[side],
            send_sem=halo_send_sem.at[side],
            recv_sem=halo_recv_sem.at[side],
            device_id=(me_g, owner),
            device_id_type=MESH,
        )

    @pl.when(me_o < n_o - 1)
    def _():
        halo_copy(0, me_o + 1).start()

    @pl.when(me_o > 0)
    def _():
        halo_copy(1, me_o - 1).start()

    def sent(k, carry):
        copy_to(k).wait_send()
        return carry

    lax.fori_loop(1, n, sent, 0)

    @pl.when(me_o > 0)
    def _():
        halo_copy(0, me_o - 1).wait_recv()

    @pl.when(me_o < n_o - 1)
    def _():
        halo_copy(1, me_o + 1).wait_recv()

    ext[0:REACH, :] = halo_in[0].astype(jnp.float32)
    ext[REACH + STRIP :, :] = halo_in[1].astype(jnp.float32)

    def smooth(j, carry):
        start = pl.multiple_of(j * CHUNK, 128)
        rows = [ext[a : a + STRIP, pl.ds(start, CHUNK + 128)] for a in range(TAPS)]
        total = None
        for b in range(TAPS):
            part = rows[0] * kern_ref[0, b]
            for a in range(1, TAPS):
                part = part + rows[a] * kern_ref[a, b]
            part = part[:, b : b + CHUNK]
            total = part if total is None else total + part
        out_ref[:, pl.ds(start, CHUNK)] = total
        return carry

    lax.fori_loop(0, quarter // CHUNK, smooth, 0)

    @pl.when(me_o < n_o - 1)
    def _():
        halo_copy(0, me_o + 1).wait_send()

    @pl.when(me_o > 0)
    def _():
        halo_copy(1, me_o - 1).wait_send()


def per_device(tile_row, pixel_col, weight, counts, kernel):
    n_o = lax.axis_size("own")
    n_g = lax.axis_size("grp")
    n = n_g * n_o
    slots = tile_row.shape[2]
    cap = slots // n_o
    quarter = W // n_g
    span = -(-(max(o * cap % 128 for o in range(n_o)) + cap) // 128) * 128
    tiles = -(-(quarter + 2 * REACH) // LANES)
    width = tiles * LANES
    vmem = pl.BlockSpec(memory_space=pltpu.VMEM)
    smem = pl.BlockSpec(memory_space=pltpu.SMEM)
    return pl.pallas_call(
        functools.partial(heat_kernel, n_g, n_o, cap, span),
        out_shape=jax.ShapeDtypeStruct((STRIP, quarter), jnp.float32),
        in_specs=[vmem, vmem, vmem, smem, smem],
        out_specs=vmem,
        scratch_shapes=[
            pltpu.VMEM((2, slots), jnp.float32),
            pltpu.VMEM((n, 2, span), jnp.float32),
            pltpu.VMEM((tiles * STRIP, LANES), jnp.float32),
            pltpu.VMEM((2, REACH, width), jnp.bfloat16),
            pltpu.VMEM((2, REACH, width), jnp.bfloat16),
            pltpu.VMEM((STRIP + 2 * REACH, width), jnp.float32),
            pltpu.SemaphoreType.DMA((n,)),
            pltpu.SemaphoreType.DMA((n,)),
            pltpu.SemaphoreType.DMA((2,)),
            pltpu.SemaphoreType.DMA((2,)),
        ],
        compiler_params=pltpu.CompilerParams(collective_id=0, has_side_effects=True),
    )(tile_row, pixel_col, weight, counts, kernel)


def solution(mesh):
    placed = (
        P("grp", "own", None),
        P("grp", "own", None),
        P("grp", "own", None),
        P("grp", "own", None),
        P(),
    )
    return jax.shard_map(
        per_device, mesh=mesh, in_specs=placed, out_specs=P("own", "grp"), check_vma=False
    )
```

time: 112 us -> 21.5 us (0.19)
  other arithmetic: 58.2 us -> 0 us
  starting transfers between devices: 28 us -> 0 us
  Pallas kernels: 0 us -> 19.7 us
  waiting for transfers between devices: 17 us -> 0 us
  local copies, waits for them, and re-layouts: 5.53 us -> 1.57 us
  matrix products: 1.92 us -> 0 us
    add x3 -> x0, other arithmetic: 54.6 us -> none  [the longest x1 53.9 us: per_device(): smoothed = smoothed + kernel[a, b] * framed[a:a + STRIP, b:b + quarter_cols]]
    pallas_call x0 -> x1, Pallas kernels: none -> 19.7 us  [per_device(): pl.pallas_call(functools.partial(heat_kernel, n_g, n_o, cap, span), out_s...]
    all_to_all x4 -> x0, starting transfers between devices: 19.6 us -> none  [the longest x1 8.13 us: per_device(): lax.all_to_all(lax.all_to_all(sent_masses, 'grp', split_axis=0, concat_ax...]
    all_to_all x4 -> x0, waiting for transfers between devices: 12.1 us -> none  [the longest x1 4.17 us: per_device(): lax.all_to_all(lax.all_to_all(sent_index, 'grp', split_axis=0, concat_axi...]
    ppermute x4 -> x0, starting transfers between devices: 8.42 us -> none  [the longest x2 5.21 us: extended(): lax.ppermute(tail, axis, [(i, (i + 1) % count) for i in range(ends)])]
    ppermute x4 -> x0, waiting for transfers between devices: 4.91 us -> none  [the longest x2 4.91 us: extended(): lax.ppermute(head, axis, [((i + 1) % count, i) for i in range(ends)])]
    slice x9 -> x0, local copies, waits for them, and re-layouts: 3.68 us -> none  [the longest x5 3.56 us: per_device(): smoothed = smoothed + kernel[a, b] * framed[a:a + STRIP, b:b + quarter_cols]]
    dot_general x1 -> x0, matrix products: 1.92 us -> none  [add_block(): jnp.dot(onehot_cells, onehot_lanes, preferred_element_type=jnp.float32)]
  transfers between devices with their start and end apart: 8 -> 0, of which waited for: 6 -> 0; matrix products, arithmetic and copies ran while one was open for 6% -> 0% of each run, Pallas kernels for 0% -> 0%
where the time goes in v1:
time: 21.5 us; the launch traced here: 21.3 us
  Pallas kernels  19.7 us (92%)
  local copies, waits for them, and re-layouts  1.57 us (7%)
    pallas_call x1, Pallas kernels, per_device(): pl.pallas_call(functools.partial(heat_kernel, n_g, n_o, cap, span), out_s...  19.7 us
    unnamed x1, local copies, waits for them, and re-layouts  1.57 us

profile of v1, /device:TPU:1, one launch (start us, length us, event | category | flops | bytes accessed | tf_op | source)
XLA Modules:
  0.0 21.3 jit_solution(798138226229270729)
XLA Ops:
  0.0 19.7 %shard_map.55 = f32[8,4096]{1,0:T(8,128)} custom-call(s32[1,1,1536]{2,1,0:T(1,128)} %row_ref.1, s32[1,1,1536]{2,1,0:T(1,128)} %col_ref.1, bf16[1,1,1536]{2,1,0:T(2,128)(2,1)} %weight_ref.1, s32[1,1,8]{2,1,0:T(1,128)} %counts_ref.1, f32[9,9]{1,0:T(8,128)} %kern_ref.1), custom_call_target="tpu_custom_call" | custom-call | tf_op jit(solution)/shard_map/pallas_call | solution.py:221
  19.7 1.6 %copy.7 = f32[8,4096]{1,0:T(8,128)} copy(f32[8,4096]{1,0:T(8,128)} %shard_map.55) | data formatting | bytes 262144

commit v2 on v1

--- a/solution.py
+++ b/solution.py
@@ -19,9 +19,10 @@
 
 
 def heat_kernel(
-    n_g, n_o, cap, span, row_ref, col_ref, weight_ref, counts_ref, kern_ref, out_ref,
-    stage, recv, acc, halo_out, halo_in, ext,
-    send_sem, recv_sem, halo_send_sem, halo_recv_sem,
+    n_g, n_o, cap, span, row_hbm, col_hbm, weight_hbm, counts_hbm, kern_hbm, out_ref,
+    row_ref, col_ref, weight_ref, counts_ref, kern_ref,
+    stage, recv, acc, halo_out, halo_in, ext, edge, edge_taps,
+    load_sem, send_sem, recv_sem, halo_send_sem, halo_recv_sem,
 ):
     n = n_g * n_o
     me_g, me_o = lax.axis_index("grp"), lax.axis_index("own")
@@ -30,6 +31,21 @@
     slots = row_ref.shape[2]
     tiles = acc.shape[0] // STRIP
 
+    loads = [
+        pltpu.make_async_copy(source, target, load_sem.at[k])
+        for k, (source, target) in enumerate(
+            [
+                (row_hbm, row_ref),
+                (col_hbm, col_ref),
+                (weight_hbm, weight_ref),
+                (counts_hbm, counts_ref),
+                (kern_hbm, kern_ref),
+            ]
+        )
+    ]
+    for load in loads:
+        load.start()
+
     barrier = pltpu.get_barrier_semaphore()
 
     def greet(k, carry):
@@ -40,6 +56,9 @@
         return carry
 
     lax.fori_loop(1, n, greet, 0)
+
+    for load in loads:
+        load.wait()
 
     period = math.lcm(cap, 128)
     per = period // cap
@@ -64,13 +83,33 @@
             halo_in[k] = halo_in_zero
 
     acc[...] = jnp.zeros_like(acc)
+    ext[...] = jnp.zeros_like(ext)
+    edge[...] = jnp.zeros_like(edge)
+    upper = lax.broadcasted_iota(jnp.int32, (STRIP, 128), 0) < REACH
+    for a in range(REACH):
+        for b in range(TAPS):
+            edge_taps[a * TAPS + b] = jnp.where(upper, kern_ref[a, b], kern_ref[a + REACH + 1, b])
+
+    def partner(t):
+        if n_o & (n_o - 1):
+            return lax.rem(me_o + t, n_o)
+        place, bit = 0, 1
+        while bit < n_o:
+            place = place + bit * lax.rem(lax.div(me_o, bit) + lax.div(t, bit), 2)
+            bit *= 2
+        return place
+
+    def peer_of(k):
+        return lax.rem(me_g + lax.rem(k, n_g), n_g), partner(lax.div(k, n_g))
+
+    def source_of(k):
+        return lax.rem(me_g + lax.rem(k, n_g), n_g), partner(lax.div(k, n_g))
 
     def window(owner):
         return pl.ds(pl.multiple_of(lax.div(owner * cap, 128) * 128, 128), span)
 
     def copy_to(k):
-        peer = lax.rem(me + k, n)
-        peer_g, peer_o = lax.div(peer, n_o), lax.rem(peer, n_o)
+        peer_g, peer_o = peer_of(k)
         return pltpu.make_async_remote_copy(
             src_ref=stage.at[:, window(peer_o)],
             dst_ref=recv.at[me],
@@ -81,13 +120,14 @@
         )
 
     def copy_from(k):
-        src = lax.rem(me + k, n)
+        src_g, src_o = source_of(k)
+        src = src_g * n_o + src_o
         return pltpu.make_async_remote_copy(
             src_ref=stage.at[:, window(me_o)],
             dst_ref=recv.at[src],
             send_sem=send_sem.at[k],
             recv_sem=recv_sem.at[src],
-            device_id=(lax.div(src, n_o), lax.rem(src, n_o)),
+            device_id=(src_g, src_o),
             device_id_type=MESH,
         )
 
@@ -127,7 +167,8 @@
                 copy_from(k).wait_recv()
 
         for u in range(BATCH):
-            a, b = onehots(recv[lax.rem(me + t * BATCH + u, n)])
+            src_g, src_o = source_of(t * BATCH + u)
+            a, b = onehots(recv[src_g * n_o + src_o])
             cells.append(a)
             lanes.append(b)
         acc[...] += lax.dot_general(
@@ -170,17 +211,6 @@
         return carry
 
     lax.fori_loop(1, n, sent, 0)
-
-    @pl.when(me_o > 0)
-    def _():
-        halo_copy(0, me_o - 1).wait_recv()
-
-    @pl.when(me_o < n_o - 1)
-    def _():
-        halo_copy(1, me_o + 1).wait_recv()
-
-    ext[0:REACH, :] = halo_in[0].astype(jnp.float32)
-    ext[REACH + STRIP :, :] = halo_in[1].astype(jnp.float32)
 
     def smooth(j, carry):
         start = pl.multiple_of(j * CHUNK, 128)
@@ -197,6 +227,33 @@
 
     lax.fori_loop(0, quarter // CHUNK, smooth, 0)
 
+    @pl.when(me_o > 0)
+    def _():
+        halo_copy(0, me_o - 1).wait_recv()
+
+    @pl.when(me_o < n_o - 1)
+    def _():
+        halo_copy(1, me_o + 1).wait_recv()
+
+    edge[0:REACH, :] = halo_in[0].astype(jnp.float32)
+    edge[STRIP - 1 : STRIP - 1 + REACH, :] = halo_in[1].astype(jnp.float32)
+
+    def smooth_edge(j, carry):
+        start = pl.multiple_of(j * CHUNK, 128)
+        rows = [edge[a : a + STRIP, pl.ds(start, CHUNK + 128)] for a in range(REACH)]
+        total = out_ref[:, pl.ds(start, CHUNK)]
+        for b in range(TAPS):
+            part = None
+            for a in range(REACH):
+                taps = jnp.concatenate([edge_taps[a * TAPS + b]] * (CHUNK // 128 + 1), axis=1)
+                term = rows[a] * taps
+                part = term if part is None else part + term
+            total = total + part[:, b : b + CHUNK]
+        out_ref[:, pl.ds(start, CHUNK)] = total
+        return carry
+
+    lax.fori_loop(0, quarter // CHUNK, smooth_edge, 0)
+
     @pl.when(me_o < n_o - 1)
     def _():
         halo_copy(0, me_o + 1).wait_send()
@@ -217,19 +274,27 @@
     tiles = -(-(quarter + 2 * REACH) // LANES)
     width = tiles * LANES
     vmem = pl.BlockSpec(memory_space=pltpu.VMEM)
-    smem = pl.BlockSpec(memory_space=pltpu.SMEM)
+    hbm = pl.BlockSpec(memory_space=pltpu.HBM)
     return pl.pallas_call(
         functools.partial(heat_kernel, n_g, n_o, cap, span),
-        out_shape=jax.ShapeDtypeStruct((STRIP, quarter), jnp.float32),
-        in_specs=[vmem, vmem, vmem, smem, smem],
+        out_shape=pltpu.VMEM((STRIP, quarter), jnp.float32),
+        in_specs=[hbm] * 5,
         out_specs=vmem,
         scratch_shapes=[
+            pltpu.VMEM(tile_row.shape, jnp.int32),
+            pltpu.VMEM(pixel_col.shape, jnp.int32),
+            pltpu.VMEM(weight.shape, weight.dtype),
+            pltpu.SMEM(counts.shape, jnp.int32),
+            pltpu.SMEM(kernel.shape, jnp.float32),
             pltpu.VMEM((2, slots), jnp.float32),
             pltpu.VMEM((n, 2, span), jnp.float32),
             pltpu.VMEM((tiles * STRIP, LANES), jnp.float32),
             pltpu.VMEM((2, REACH, width), jnp.bfloat16),
             pltpu.VMEM((2, REACH, width), jnp.bfloat16),
             pltpu.VMEM((STRIP + 2 * REACH, width), jnp.float32),
+            pltpu.VMEM((STRIP + 2 * REACH, width), jnp.float32),
+            pltpu.VMEM((REACH * TAPS, STRIP, 128), jnp.float32),
+            pltpu.SemaphoreType.DMA((5,)),
             pltpu.SemaphoreType.DMA((n,)),
             pltpu.SemaphoreType.DMA((n,)),
             pltpu.SemaphoreType.DMA((2,)),

time: 21.5 us -> 18.4 us (0.86)
  the two profiles are of different devices: /device:TPU:1 before, /device:TPU:0 now
where the time goes in v2:
time: 18.4 us; the launch traced here: 18.2 us
  Pallas kernels  17.5 us (95%)
  local copies, waits for them, and re-layouts  0.66 us (4%)
    pallas_call x1, Pallas kernels, per_device(): pl.pallas_call(functools.partial(heat_kernel, n_g, n_o, cap, span), out_s...  17.5 us
    unnamed x1, local copies, waits for them, and re-layouts  0.66 us

profile of v2, /device:TPU:0, one launch (start us, length us, event | category | flops | bytes accessed | tf_op | source)
XLA Modules:
  0.0 18.2 jit_solution(12153874389401272950)
XLA Ops:
  0.0 17.5 %shard_map.55 = f32[8,4096]{1,0:T(8,128)S(1)} custom-call(s32[1,1,1536]{2,1,0:T(1,128)} %row_hbm.1, s32[1,1,1536]{2,1,0:T(1,128)} %col_hbm.1, bf16[1,1,1536]{2,1,0:T(2,128)(2,1)} %weight_hbm.1, s32[1,1,8]{2,1,0:T(1,128)} %counts_hbm.1, f32[9,9]{1,0:T(8,128)} %kern_hbm.1), custom_call_target="tpu_custom_call" | custom-call | tf_op jit(solution)/shard_map/pallas_call | solution.py:278
  17.5 0.7 %copy.7 = f32[8,4096]{1,0:T(8,128)} copy(f32[8,4096]{1,0:T(8,128)S(1)} %shard_map.55) | data formatting | bytes 262144

commit v3 on v2

--- a/solution.py
+++ b/solution.py
@@ -14,19 +14,17 @@
 TAPS = 9
 LANES = 256
 CHUNK = 512
-BATCH = 4
 MESH = pl.DeviceIdType.MESH
 
 
 def heat_kernel(
     n_g, n_o, cap, span, row_hbm, col_hbm, weight_hbm, counts_hbm, kern_hbm, out_ref,
     row_ref, col_ref, weight_ref, counts_ref, kern_ref,
-    stage, recv, acc, halo_out, halo_in, ext, edge, edge_taps,
+    stage, recv, acc, halo_out, halo_in, own_rows, edge_rows, edge_taps,
     load_sem, send_sem, recv_sem, halo_send_sem, halo_recv_sem,
 ):
     n = n_g * n_o
     me_g, me_o = lax.axis_index("grp"), lax.axis_index("own")
-    me = me_g * n_o + me_o
     quarter = out_ref.shape[1]
     slots = row_ref.shape[2]
     tiles = acc.shape[0] // STRIP
@@ -48,14 +46,37 @@
 
     barrier = pltpu.get_barrier_semaphore()
 
-    def greet(k, carry):
-        peer = lax.rem(me + k, n)
-        pl.semaphore_signal(
-            barrier, inc=1, device_id=(lax.div(peer, n_o), lax.rem(peer, n_o)), device_id_type=MESH
-        )
-        return carry
-
-    lax.fori_loop(1, n, greet, 0)
+    def offset_place(mine, step, count):
+        if count & (count - 1):
+            return lax.rem(mine + step, count)
+        place, bit = 0, 1
+        while bit < count:
+            place = place + bit * lax.rem(lax.div(mine, bit) + lax.div(step, bit), 2)
+            bit *= 2
+        return place
+
+    def mirrored(step, count):
+        return lax.rem(count - step, count) if count & (count - 1) else step
+
+    groups = [offset_place(me_g, jnp.int32(u), n_g) for u in range(n_g)]
+
+    def farthest_first(act):
+        def ring(r, carry):
+            step = n_o - 1 - r
+            owner = offset_place(me_o, step, n_o)
+            for u in range(n_g):
+                act(step, u, owner)
+            return carry
+
+        lax.fori_loop(0, n_o - 1, ring, 0)
+        for u in range(1, n_g):
+            act(0, u, me_o)
+
+    farthest_first(
+        lambda step, u, owner: pl.semaphore_signal(
+            barrier, inc=1, device_id=(groups[u], owner), device_id_type=MESH
+        )
+    )
 
     for load in loads:
         load.wait()
@@ -83,62 +104,39 @@
             halo_in[k] = halo_in_zero
 
     acc[...] = jnp.zeros_like(acc)
-    ext[...] = jnp.zeros_like(ext)
-    edge[...] = jnp.zeros_like(edge)
     upper = lax.broadcasted_iota(jnp.int32, (STRIP, 128), 0) < REACH
     for a in range(REACH):
         for b in range(TAPS):
             edge_taps[a * TAPS + b] = jnp.where(upper, kern_ref[a, b], kern_ref[a + REACH + 1, b])
 
-    def partner(t):
-        if n_o & (n_o - 1):
-            return lax.rem(me_o + t, n_o)
-        place, bit = 0, 1
-        while bit < n_o:
-            place = place + bit * lax.rem(lax.div(me_o, bit) + lax.div(t, bit), 2)
-            bit *= 2
-        return place
-
-    def peer_of(k):
-        return lax.rem(me_g + lax.rem(k, n_g), n_g), partner(lax.div(k, n_g))
-
-    def source_of(k):
-        return lax.rem(me_g + lax.rem(k, n_g), n_g), partner(lax.div(k, n_g))
-
     def window(owner):
         return pl.ds(pl.multiple_of(lax.div(owner * cap, 128) * 128, 128), span)
 
-    def copy_to(k):
-        peer_g, peer_o = peer_of(k)
+    def copy(step, u, owner):
+        there = mirrored(step, n_o) * n_g + mirrored(u, n_g)
         return pltpu.make_async_remote_copy(
-            src_ref=stage.at[:, window(peer_o)],
-            dst_ref=recv.at[me],
+            src_ref=stage.at[:, window(owner)],
+            dst_ref=recv.at[there],
+            send_sem=send_sem.at[step * n_g + u],
+            recv_sem=recv_sem.at[there],
+            device_id=(groups[u], owner),
+            device_id_type=MESH,
+        )
+
+    def arrival(k):
+        return pltpu.make_async_remote_copy(
+            src_ref=recv.at[k],
+            dst_ref=recv.at[k],
             send_sem=send_sem.at[k],
-            recv_sem=recv_sem.at[me],
-            device_id=(peer_g, peer_o),
+            recv_sem=recv_sem.at[k],
+            device_id=(me_g, me_o),
             device_id_type=MESH,
         )
 
-    def copy_from(k):
-        src_g, src_o = source_of(k)
-        src = src_g * n_o + src_o
-        return pltpu.make_async_remote_copy(
-            src_ref=stage.at[:, window(me_o)],
-            dst_ref=recv.at[src],
-            send_sem=send_sem.at[k],
-            recv_sem=recv_sem.at[src],
-            device_id=(src_g, src_o),
-            device_id_type=MESH,
-        )
-
     pl.semaphore_wait(barrier, n - 1)
 
-    def send(k, carry):
-        copy_to(k).start()
-        return carry
-
-    lax.fori_loop(1, n, send, 0)
-    recv[me] = stage[:, window(me_o)]
+    farthest_first(lambda step, u, owner: copy(step, u, owner).start())
+    recv[0] = stage[:, window(me_o)]
 
     offset = lax.rem(me_o * cap, 128)
     first_col = me_g * quarter - REACH
@@ -159,16 +157,16 @@
 
     def bin_batch(t, carry):
         cells, lanes = [], []
-        for u in range(BATCH):
-            k = t * BATCH + u
-
-            @pl.when(k > 0)
-            def _():
-                copy_from(k).wait_recv()
-
-        for u in range(BATCH):
-            src_g, src_o = source_of(t * BATCH + u)
-            a, b = onehots(recv[src_g * n_o + src_o])
+        for u in range(n_g):
+            if u == 0:
+
+                @pl.when(t > 0)
+                def _():
+                    arrival(t * n_g).wait_recv()
+            else:
+                arrival(t * n_g + u).wait_recv()
+        for u in range(n_g):
+            a, b = onehots(recv[t * n_g + u])
             cells.append(a)
             lanes.append(b)
         acc[...] += lax.dot_general(
@@ -179,14 +177,13 @@
         )
         return carry
 
-    lax.fori_loop(0, n // BATCH, bin_batch, 0)
+    lax.fori_loop(0, n_o, bin_batch, 0)
 
     for t in range(tiles):
         at = pl.ds(t * LANES, LANES)
         heat = acc[t * STRIP : (t + 1) * STRIP, :]
         halo_out[0, :, at] = heat[STRIP - REACH :].astype(jnp.bfloat16)
         halo_out[1, :, at] = heat[:REACH].astype(jnp.bfloat16)
-        ext[REACH : REACH + STRIP, at] = heat
 
     def halo_copy(side, owner):
         return pltpu.make_async_remote_copy(
@@ -207,14 +204,25 @@
         halo_copy(1, me_o - 1).start()
 
     def sent(k, carry):
-        copy_to(k).wait_send()
+        arrival(k).wait_send()
         return carry
 
     lax.fori_loop(1, n, sent, 0)
+
+    blank = jnp.zeros((REACH, LANES), jnp.float32)
+
+    def shift_own(t, carry):
+        heat = acc[pl.ds(pl.multiple_of(t * STRIP, STRIP), STRIP), :]
+        framed = jnp.concatenate([blank, heat, blank], axis=0)
+        for a in range(TAPS):
+            own_rows[a, :, pl.ds(pl.multiple_of(t * LANES, LANES), LANES)] = framed[a : a + STRIP]
+        return carry
+
+    lax.fori_loop(0, tiles, shift_own, 0)
 
     def smooth(j, carry):
         start = pl.multiple_of(j * CHUNK, 128)
-        rows = [ext[a : a + STRIP, pl.ds(start, CHUNK + 128)] for a in range(TAPS)]
+        rows = [own_rows[a, :, pl.ds(start, CHUNK + 128)] for a in range(TAPS)]
         total = None
         for b in range(TAPS):
             part = rows[0] * kern_ref[0, b]
@@ -235,12 +243,20 @@
     def _():
         halo_copy(1, me_o + 1).wait_recv()
 
-    edge[0:REACH, :] = halo_in[0].astype(jnp.float32)
-    edge[STRIP - 1 : STRIP - 1 + REACH, :] = halo_in[1].astype(jnp.float32)
+    def shift_edge(t, carry):
+        at = pl.ds(pl.multiple_of(t * LANES, LANES), LANES)
+        above = halo_in[0, :, at].astype(jnp.float32)
+        below = halo_in[1, :, at].astype(jnp.float32)
+        framed = jnp.concatenate([above, blank[: REACH - 1], below], axis=0)
+        for a in range(REACH):
+            edge_rows[a, :, at] = framed[a : a + STRIP]
+        return carry
+
+    lax.fori_loop(0, tiles, shift_edge, 0)
 
     def smooth_edge(j, carry):
         start = pl.multiple_of(j * CHUNK, 128)
-        rows = [edge[a : a + STRIP, pl.ds(start, CHUNK + 128)] for a in range(REACH)]
+        rows = [edge_rows[a, :, pl.ds(start, CHUNK + 128)] for a in range(REACH)]
         total = out_ref[:, pl.ds(start, CHUNK)]
         for b in range(TAPS):
             part = None
@@ -291,8 +307,8 @@
             pltpu.VMEM((tiles * STRIP, LANES), jnp.float32),
             pltpu.VMEM((2, REACH, width), jnp.bfloat16),
             pltpu.VMEM((2, REACH, width), jnp.bfloat16),
-            pltpu.VMEM((STRIP + 2 * REACH, width), jnp.float32),
-            pltpu.VMEM((STRIP + 2 * REACH, width), jnp.float32),
+            pltpu.VMEM((TAPS, STRIP, width), jnp.float32),
+            pltpu.VMEM((REACH, STRIP, width), jnp.float32),
             pltpu.VMEM((REACH * TAPS, STRIP, 128), jnp.float32),
             pltpu.SemaphoreType.DMA((5,)),
             pltpu.SemaphoreType.DMA((n,)),

time: 18.4 us -> 17 us (0.924)
  the two profiles are of different devices: /device:TPU:0 before, /device:TPU:1 now
where the time goes in v3:
time: 17 us; the launch traced here: 16.8 us
  Pallas kernels  16.1 us (95%)
  local copies, waits for them, and re-layouts  0.66 us (4%)
    pallas_call x1, Pallas kernels, per_device(): pl.pallas_call(functools.partial(heat_kernel, n_g, n_o, cap, span), out_s...  16.1 us
    unnamed x1, local copies, waits for them, and re-layouts  0.66 us

profile of v3, /device:TPU:1, one launch (start us, length us, event | category | flops | bytes accessed | tf_op | source)
XLA Modules:
  0.0 16.8 jit_solution(13067337024947066040)
XLA Ops:
  0.0 16.1 %shard_map.55 = f32[8,4096]{1,0:T(8,128)S(1)} custom-call(s32[1,1,1536]{2,1,0:T(1,128)} %row_hbm.1, s32[1,1,1536]{2,1,0:T(1,128)} %col_hbm.1, bf16[1,1,1536]{2,1,0:T(2,128)(2,1)} %weight_hbm.1, s32[1,1,8]{2,1,0:T(1,128)} %counts_hbm.1, f32[9,9]{1,0:T(8,128)} %kern_hbm.1), custom_call_target="tpu_custom_call" | custom-call | tf_op jit(solution)/shard_map/pallas_call | solution.py:294
  16.1 0.7 %copy.7 = f32[8,4096]{1,0:T(8,128)} copy(f32[8,4096]{1,0:T(8,128)S(1)} %shard_map.55) | data formatting | bytes 262144

commit v4 on v3

--- a/solution.py
+++ b/solution.py
@@ -149,10 +149,13 @@
         mass = jnp.where(used, points[1:2], 0.0)
         cell = (reach // LANES) * STRIP + index // W
         lane = reach & (LANES - 1)
-        cell_iota = lax.broadcasted_iota(jnp.int32, (acc.shape[0], span), 0)
-        lane_iota = lax.broadcasted_iota(jnp.int32, (LANES, span), 0)
-        cells = jnp.where(cell_iota == cell, 1.0, 0.0).astype(jnp.bfloat16)
-        lanes = jnp.where(lane_iota == lane, mass, 0.0).astype(jnp.bfloat16)
+        half = jnp.bfloat16
+        cell = jnp.where(used, cell, 0).astype(jnp.float32).astype(half)
+        lane = lane.astype(jnp.float32).astype(half)
+        cell_iota = lax.broadcasted_iota(jnp.int32, (acc.shape[0], span), 0).astype(jnp.float32).astype(half)
+        lane_iota = lax.broadcasted_iota(jnp.int32, (LANES, span), 0).astype(jnp.float32).astype(half)
+        cells = jnp.where(cell_iota == cell, half(1), half(0))
+        lanes = jnp.where(lane_iota == lane, mass.astype(half), half(0))
         return cells, lanes
 
     def bin_batch(t, carry):

time: 17 us -> 16.9 us (level)
  no operation moved by 1% of the time
where the time goes in v4:
time: 16.9 us; the launch traced here: 16.8 us
  Pallas kernels  16.1 us (95%)
  local copies, waits for them, and re-layouts  0.66 us (4%)
    pallas_call x1, Pallas kernels, per_device(): pl.pallas_call(functools.partial(heat_kernel, n_g, n_o, cap, span), out_s...  16.1 us
    unnamed x1, local copies, waits for them, and re-layouts  0.66 us

profile of v4, /device:TPU:1, one launch (start us, length us, event | category | flops | bytes accessed | tf_op | source)
XLA Modules:
  0.0 16.8 jit_solution(10163953537592873997)
XLA Ops:
  0.0 16.1 %shard_map.55 = f32[8,4096]{1,0:T(8,128)S(1)} custom-call(s32[1,1,1536]{2,1,0:T(1,128)} %row_hbm.1, s32[1,1,1536]{2,1,0:T(1,128)} %col_hbm.1, bf16[1,1,1536]{2,1,0:T(2,128)(2,1)} %weight_hbm.1, s32[1,1,8]{2,1,0:T(1,128)} %counts_hbm.1, f32[9,9]{1,0:T(8,128)} %kern_hbm.1), custom_call_target="tpu_custom_call" | custom-call | tf_op jit(solution)/shard_map/pallas_call | solution.py:297
  16.1 0.7 %copy.7 = f32[8,4096]{1,0:T(8,128)} copy(f32[8,4096]{1,0:T(8,128)S(1)} %shard_map.55) | data formatting | bytes 262144

commit v5 on v4

--- a/solution.py
+++ b/solution.py
@@ -13,7 +13,7 @@
 REACH = 4
 TAPS = 9
 LANES = 256
-CHUNK = 512
+CHUNK = 1024
 MESH = pl.DeviceIdType.MESH
 
 
@@ -64,7 +64,7 @@
         def ring(r, carry):
             step = n_o - 1 - r
             owner = offset_place(me_o, step, n_o)
-            for u in range(n_g):
+            for u in reversed(range(n_g)):
                 act(step, u, owner)
             return carry
 

time: 16.9 us -> 16.6 us (0.982)
  Pallas kernels: 16.1 us -> 15.8 us
    pallas_call x1, Pallas kernels: 16.1 us -> 15.8 us  [per_device(): pl.pallas_call(functools.partial(heat_kernel, n_g, n_o, cap, span), out_s...]
where the time goes in v5:
time: 16.6 us; the launch traced here: 16.4 us
  Pallas kernels  15.8 us (95%)
  local copies, waits for them, and re-layouts  0.66 us (4%)
    pallas_call x1, Pallas kernels, per_device(): pl.pallas_call(functools.partial(heat_kernel, n_g, n_o, cap, span), out_s...  15.8 us
    unnamed x1, local copies, waits for them, and re-layouts  0.66 us

profile of v5, /device:TPU:1, one launch (start us, length us, event | category | flops | bytes accessed | tf_op | source)
XLA Modules:
  0.0 16.4 jit_solution(1198471867906945226)
XLA Ops:
  0.0 15.8 %shard_map.55 = f32[8,4096]{1,0:T(8,128)S(1)} custom-call(s32[1,1,1536]{2,1,0:T(1,128)} %row_hbm.1, s32[1,1,1536]{2,1,0:T(1,128)} %col_hbm.1, bf16[1,1,1536]{2,1,0:T(2,128)(2,1)} %weight_hbm.1, s32[1,1,8]{2,1,0:T(1,128)} %counts_hbm.1, f32[9,9]{1,0:T(8,128)} %kern_hbm.1), custom_call_target="tpu_custom_call" | custom-call | tf_op jit(solution)/shard_map/pallas_call | solution.py:297
  15.8 0.7 %copy.7 = f32[8,4096]{1,0:T(8,128)} copy(f32[8,4096]{1,0:T(8,128)S(1)} %shard_map.55) | data formatting | bytes 262144
